TPU v7x, 32 devices: a whole 2x2x4 slice. The times are simulated.
32 devices in a mesh: grp: 8 (over z, x), seq: 4 (over y, core).
Axes of the slice: x: 2, y: 2, z: 4, core: 2. Of those that a mesh axis runs over, the one named last changes fastest.
Arguments:
- inputs: bfloat16 [2, 8, 512, 1536], P(None, 'grp', 'seq'), may hold values from -6 to 6
- cont_lengths: int32 [2, 8, 2], P(None, 'grp'), may hold values from 1 to 256, 448 in all within a row
- w_query: bfloat16 [1536, 1536], P(('grp', 'seq')), may hold values from -0.15625 to 0.15625
- key_projection: bfloat16 [1536, 768], P(('grp', 'seq')), may hold values from -0.15625 to 0.15625
- value_projection: bfloat16 [1536, 768], P(('grp', 'seq')), may hold values from -0.15625 to 0.15625
- w_out: bfloat16 [1536, 1536], P(None, ('grp', 'seq')), may hold values from -1.75 to 1.75
- attn_gain: bfloat16 [1536], P(('grp', 'seq')), may hold values from 0.25 to 1.75
- w_gate: bfloat16 [1536, 4096], P(('grp', 'seq')), may hold values from -0.15625 to 0.15625
- w_up: bfloat16 [1536, 4096], P(('grp', 'seq')), may hold values from -0.15625 to 0.15625
- w_down: bfloat16 [4096, 1536], P(('grp', 'seq')), may hold values from -0.09375 to 0.09375
- mlp_gain: bfloat16 [1536], P(('grp', 'seq')), may hold values from 0.25 to 1.75
- cotangent: bfloat16 [2, 8, 512, 1536], P(None, 'grp', 'seq'), may hold values from -6 to 6
Outputs:
- outputs: bfloat16 [2, 8, 512, 1536], P(None, 'grp', 'seq')
- grad_inputs: float32 [2, 8, 512, 1536], P(None, 'grp', 'seq')
- grad_query: float32 [1536, 1536], P(('grp', 'seq'))
- grad_key: float32 [1536, 768], P(('grp', 'seq'))
- grad_value: float32 [1536, 768], P(('grp', 'seq'))
- grad_out: float32 [1536, 1536], P(None, ('grp', 'seq'))
- grad_attn_gain: float32 [1536], P(('grp', 'seq'))
- grad_gate: float32 [1536, 4096], P(('grp', 'seq'))
- grad_up: float32 [1536, 4096], P(('grp', 'seq'))
- grad_down: float32 [4096, 1536], P(('grp', 'seq'))
- grad_mlp_gain: float32 [1536], P(('grp', 'seq'))
Inputs may be any that keep to these rules, and one draw needn't show every extreme that they name: `cont_lengths`: each group's 2 continuation lengths sum to 448.
All inputs are finite; a program needn't handle non-finite values.
Results may differ from a plain program's by a relative error of at most 0.017.
Values may be sent and summed in bfloat16 or wider, within the bound.
A program may use at most 320 MiB of HBM per device.

v0:
```python
import jax
import jax.numpy as jnp
from jax import lax
from jax.sharding import PartitionSpec as P

QUERY_HEADS = 16
KEY_VALUE_HEADS = 8
HEAD_SIZE = 96
CONT_MEAN = 224


EPSILON = 1e-05
ROPE_BASE = 100000.0
MASK_FILL = -1e30


def layout(lengths, rows_per_group, prompt_rows):
    row_ids = jnp.arange(rows_per_group, dtype=jnp.int32)
    cont_ends = prompt_rows + jnp.cumsum(lengths)
    cont_starts = cont_ends - lengths
    member = (
        (row_ids[:, None] >= cont_starts[None, :]) & (row_ids[:, None] < cont_ends[None, :])
    ).astype(jnp.int32)
    labels = jnp.arange(1, lengths.shape[0] + 1, dtype=jnp.int32)
    segment = jnp.sum(member * labels[None, :], axis=1)
    offsets = jnp.sum(member * cont_starts[None, :], axis=1)
    position = jnp.where(segment > 0, prompt_rows + row_ids - offsets, row_ids)
    return (segment, position)


def rotation(position):
    half_dim = HEAD_SIZE // 2
    frequency = ROPE_BASE ** (-2.0 * jnp.arange(half_dim, dtype=jnp.float32) / HEAD_SIZE)
    angles = position.astype(jnp.float32)[:, None] * frequency[None, :]
    return (jnp.cos(angles), jnp.sin(angles))


def apply_rotary(head_values, cosine_lookup, sine_lookup):
    half_dim = head_values.shape[-1] // 2
    first_half = head_values[..., :half_dim]
    second_half = head_values[..., half_dim:]
    cos_wide = cosine_lookup[:, None, :]
    sin_wide = sine_lookup[:, None, :]
    return jnp.concatenate(
        [
            first_half * cos_wide - second_half * sin_wide,
            second_half * cos_wide + first_half * sin_wide,
        ],
        axis=-1,
    )


def inverse_rotary(head_values, cosine_lookup, sine_lookup):
    half_dim = head_values.shape[-1] // 2
    first_half = head_values[..., :half_dim]
    second_half = head_values[..., half_dim:]
    cos_wide = cosine_lookup[:, None, :]
    sin_wide = sine_lookup[:, None, :]
    return jnp.concatenate(
        [
            first_half * cos_wide + second_half * sin_wide,
            second_half * cos_wide - first_half * sin_wide,
        ],
        axis=-1,
    )


def norm_rows(row_values, gain):
    inverse = lax.rsqrt(jnp.mean(row_values * row_values, axis=-1, keepdims=True) + EPSILON)
    return (row_values * inverse * gain.astype(jnp.float32), inverse)


def norm_back(grad_normed, row_values, inverse, gain):
    scaled = grad_normed * gain.astype(jnp.float32)
    grad_gain = jnp.sum(grad_normed * row_values * inverse, axis=0)
    grad_values = inverse * scaled - row_values * inverse**3 * jnp.mean(
        scaled * row_values, axis=-1, keepdims=True
    )
    return (grad_values, grad_gain)


def inner_rows(left, right):
    return lax.dot_general(
        left, right, (((0,), (0,)), ((), ())), preferred_element_type=jnp.float32
    )


def times_transpose(left, right):
    return lax.dot_general(
        left, right, (((1,), (1,)), ((), ())), preferred_element_type=jnp.float32
    )


def reduce_attention(grad_list):
    return tuple(
        (
            lax.psum_scatter(grad_list[0], ("grp", "seq"), scatter_dimension=0, tiled=True),
            lax.psum_scatter(grad_list[1], ("grp", "seq"), scatter_dimension=0, tiled=True),
            lax.psum_scatter(grad_list[2], ("grp", "seq"), scatter_dimension=0, tiled=True),
            lax.psum_scatter(grad_list[3], ("grp", "seq"), scatter_dimension=1, tiled=True),
            lax.psum_scatter(grad_list[4], ("grp", "seq"), scatter_dimension=0, tiled=True),
        )
    )


def reduce_mlp(grad_list):
    return tuple(
        (
            lax.psum_scatter(grad_list[0], ("grp", "seq"), scatter_dimension=0, tiled=True),
            lax.psum_scatter(grad_list[1], ("grp", "seq"), scatter_dimension=0, tiled=True),
            lax.psum_scatter(grad_list[2], ("grp", "seq"), scatter_dimension=0, tiled=True),
            lax.psum_scatter(grad_list[3], ("grp", "seq"), scatter_dimension=0, tiled=True),
        )
    )


def on_device(
    inputs,
    cont_lengths,
    w_query,
    key_projection,
    value_projection,
    w_out,
    attn_gain,
    w_gate,
    w_up,
    w_down,
    mlp_gain,
    cotangent,
):
    micro_count = inputs.shape[0]
    rows_per_shard = inputs.shape[2]
    seq_count = lax.axis_size("seq")
    rows_per_group = rows_per_shard * seq_count
    cont_count = cont_lengths.shape[2]
    prompt_rows = rows_per_group - CONT_MEAN * cont_count
    head_repeat_factor = QUERY_HEADS // KEY_VALUE_HEADS
    scale = HEAD_SIZE ** (-0.5)
    first_row = lax.axis_index("seq") * rows_per_shard
    factor = 1
    while (
        factor * 2 <= seq_count
        and seq_count % (factor * 2) == 0
        and (factor * 2 * rows_per_shard <= 512)
    ):
        factor = factor * 2
    rows_of_keys = rows_per_shard * factor
    needed = (first_row + rows_per_shard - 1) // rows_of_keys + 1
    prompt_blocks = (prompt_rows + rows_of_keys - 1) // rows_of_keys
    query_full, key_full, value_full, out_full, gain_attn = (
        lax.all_gather(w_query, ("grp", "seq"), axis=0, tiled=True),
        lax.all_gather(key_projection, ("grp", "seq"), axis=0, tiled=True),
        lax.all_gather(value_projection, ("grp", "seq"), axis=0, tiled=True),
        lax.all_gather(w_out, ("grp", "seq"), axis=1, tiled=True),
        lax.all_gather(attn_gain, ("grp", "seq"), axis=0, tiled=True),
    )
    gate_full, up_full, down_full, gain_mlp = (
        lax.all_gather(w_gate, ("grp", "seq"), axis=0, tiled=True),
        lax.all_gather(w_up, ("grp", "seq"), axis=0, tiled=True),
        lax.all_gather(w_down, ("grp", "seq"), axis=0, tiled=True),
        lax.all_gather(mlp_gain, ("grp", "seq"), axis=0, tiled=True),
    )
    owned = None
    output_list = []
    grad_input_list = []
    for micro in range(micro_count):
        rows_in = inputs[micro, 0].astype(jnp.float32)
        segment_all, position_all = layout(cont_lengths[micro, 0], rows_per_group, prompt_rows)
        my_segment = lax.dynamic_slice_in_dim(segment_all, first_row, rows_per_shard, 0)
        my_position = lax.dynamic_slice_in_dim(position_all, first_row, rows_per_shard, 0)
        cosine_lookup, sine_lookup = rotation(my_position)
        cont_first = jnp.where(
            my_segment[0] > 0, first_row - (my_position[0] - prompt_rows), first_row
        )
        prompt_count = jnp.minimum(prompt_blocks, needed)
        later_start = jnp.maximum(prompt_count, cont_first // rows_of_keys)
        count_of_blocks = prompt_count + jnp.maximum(needed - later_start, 0)

        def block_start(loop_idx):
            chosen = jnp.where(
                loop_idx < prompt_count, loop_idx, later_start + loop_idx - prompt_count
            )
            return chosen * rows_of_keys

        def visible_block(row_start):
            key_segment = lax.dynamic_slice_in_dim(segment_all, row_start, rows_of_keys, 0)
            key_position = lax.dynamic_slice_in_dim(position_all, row_start, rows_of_keys, 0)
            same_seq = (key_segment[None, :] == 0) | (key_segment[None, :] == my_segment[:, None])
            return (same_seq & (key_position[None, :] <= my_position[:, None]))[None, None]

        normed_one, inverse_one = norm_rows(rows_in, gain_attn)
        act_one = normed_one.astype(jnp.bfloat16)
        query_pre = jnp.dot(act_one, query_full, preferred_element_type=jnp.float32)
        key_unrotated = jnp.dot(act_one, key_full, preferred_element_type=jnp.float32)
        value_projected = jnp.dot(act_one, value_full, preferred_element_type=jnp.float32)
        query_rows = (
            apply_rotary(
                query_pre.reshape(rows_per_shard, QUERY_HEADS, HEAD_SIZE),
                cosine_lookup,
                sine_lookup,
            )
            * scale
        ).astype(jnp.bfloat16)
        keys_own = (
            apply_rotary(
                key_unrotated.reshape(rows_per_shard, KEY_VALUE_HEADS, HEAD_SIZE),
                cosine_lookup,
                sine_lookup,
            )
            .astype(jnp.bfloat16)
            .reshape(rows_per_shard, KEY_VALUE_HEADS * HEAD_SIZE)
        )
        values_own = value_projected.astype(jnp.bfloat16)
        keys_all, values_all = (
            lax.all_gather(keys_own, "seq", axis=0, tiled=True),
            lax.all_gather(values_own, "seq", axis=0, tiled=True),
        )
        grouped_queries = query_rows.reshape(
            rows_per_shard, KEY_VALUE_HEADS, head_repeat_factor, HEAD_SIZE
        )

        def block_scores(row_start):
            key_block = lax.dynamic_slice_in_dim(keys_all, row_start, rows_of_keys, 0).reshape(
                rows_of_keys, KEY_VALUE_HEADS, HEAD_SIZE
            )
            scores = jnp.einsum(
                "rgjd,kgd->gjrk", grouped_queries, key_block, preferred_element_type=jnp.float32
            )
            return (scores, key_block)

        def pass_max(loop_idx, running):
            run_max, run_sum = running
            row_start = block_start(loop_idx)
            scores, key_block = block_scores(row_start)
            visible = visible_block(row_start)
            block_max = jnp.max(jnp.where(visible, scores, MASK_FILL), axis=-1)
            new_max = jnp.maximum(run_max, block_max)
            weights = jnp.where(visible, jnp.exp(scores - new_max[..., None]), 0.0)
            return (new_max, run_sum * jnp.exp(run_max - new_max) + jnp.sum(weights, axis=-1))

        initial_maximum = jnp.full(
            (KEY_VALUE_HEADS, head_repeat_factor, rows_per_shard), MASK_FILL, jnp.float32
        )
        initial_total = jnp.zeros(
            (KEY_VALUE_HEADS, head_repeat_factor, rows_per_shard), jnp.float32
        )
        run_max, run_sum = lax.fori_loop(
            0, count_of_blocks, pass_max, (initial_maximum, initial_total)
        )
        log_total = run_max + jnp.log(run_sum)

        def sweep_total(loop_idx, attn_acc):
            row_start = block_start(loop_idx)
            scores, key_block = block_scores(row_start)
            visible = visible_block(row_start)
            probs = jnp.where(visible, jnp.exp(scores - log_total[..., None]), 0.0).astype(
                jnp.bfloat16
            )
            value_block = lax.dynamic_slice_in_dim(values_all, row_start, rows_of_keys, 0).reshape(
                rows_of_keys, KEY_VALUE_HEADS, HEAD_SIZE
            )
            return attn_acc + jnp.einsum(
                "gjrk,kgd->rgjd", probs, value_block, preferred_element_type=jnp.float32
            )

        attn_total = lax.fori_loop(
            0,
            count_of_blocks,
            sweep_total,
            jnp.zeros(
                (rows_per_shard, KEY_VALUE_HEADS, head_repeat_factor, HEAD_SIZE), jnp.float32
            ),
        )
        attn_low = attn_total.reshape(rows_per_shard, QUERY_HEADS * HEAD_SIZE).astype(jnp.bfloat16)
        hidden = rows_in + jnp.dot(attn_low, out_full, preferred_element_type=jnp.float32)
        normed_two, inverse_two = norm_rows(hidden, gain_mlp)
        act_two = normed_two.astype(jnp.bfloat16)
        gate_pre = jnp.dot(act_two, gate_full, preferred_element_type=jnp.float32)
        up_pre = jnp.dot(act_two, up_full, preferred_element_type=jnp.float32)
        sigmoid_gate = jax.nn.sigmoid(gate_pre)
        silu_gate = gate_pre * sigmoid_gate
        mixed_act = (silu_gate * up_pre).astype(jnp.bfloat16)
        result = hidden + jnp.dot(mixed_act, down_full, preferred_element_type=jnp.float32)
        output_list.append(result.astype(jnp.bfloat16))
        cot_rows = cotangent[micro, 0]
        grad_down = inner_rows(mixed_act, cot_rows)
        grad_mixed = times_transpose(cot_rows, down_full)
        grad_gate_pre = (
            grad_mixed * up_pre * sigmoid_gate * (1.0 + gate_pre * (1.0 - sigmoid_gate))
        ).astype(jnp.bfloat16)
        grad_up_pre = (grad_mixed * silu_gate).astype(jnp.bfloat16)
        grad_gate = inner_rows(act_two, grad_gate_pre)
        grad_up = inner_rows(act_two, grad_up_pre)
        grad_act_two = times_transpose(grad_gate_pre, gate_full) + times_transpose(
            grad_up_pre, up_full
        )
        grad_hidden_norm, grad_gain_mlp = norm_back(grad_act_two, hidden, inverse_two, gain_mlp)
        grad_hidden = cot_rows.astype(jnp.float32) + grad_hidden_norm
        mlp_grads = (grad_gate, grad_up, grad_down, grad_gain_mlp)
        hidden_low = grad_hidden.astype(jnp.bfloat16)
        grad_out = inner_rows(attn_low, hidden_low)
        attention_gradient = times_transpose(hidden_low, out_full).astype(jnp.bfloat16)
        attention_gradient_groups = attention_gradient.reshape(
            rows_per_shard, KEY_VALUE_HEADS, head_repeat_factor, HEAD_SIZE
        )
        delta = jnp.transpose(
            jnp.sum(attention_gradient_groups.astype(jnp.float32) * attn_total, axis=-1), (1, 2, 0)
        )

        def pass_back(loop_idx, running):
            grad_query_acc, grad_keys_all, grad_values_all = running
            row_start = block_start(loop_idx)
            scores, key_block = block_scores(row_start)
            visible = visible_block(row_start)
            value_block = lax.dynamic_slice_in_dim(values_all, row_start, rows_of_keys, 0).reshape(
                rows_of_keys, KEY_VALUE_HEADS, HEAD_SIZE
            )
            probs = jnp.where(visible, jnp.exp(scores - log_total[..., None]), 0.0)
            grad_probs = jnp.einsum(
                "rgjd,kgd->gjrk",
                attention_gradient_groups,
                value_block,
                preferred_element_type=jnp.float32,
            )
            grad_scores = (probs * (grad_probs - delta[..., None])).astype(jnp.bfloat16)
            grad_query_acc = grad_query_acc + jnp.einsum(
                "gjrk,kgd->rgjd", grad_scores, key_block, preferred_element_type=jnp.float32
            )
            key_part = jnp.einsum(
                "gjrk,rgjd->kgd", grad_scores, grouped_queries, preferred_element_type=jnp.float32
            ).reshape(rows_of_keys, KEY_VALUE_HEADS * HEAD_SIZE)
            value_part = jnp.einsum(
                "gjrk,rgjd->kgd",
                probs.astype(jnp.bfloat16),
                attention_gradient_groups,
                preferred_element_type=jnp.float32,
            ).reshape(rows_of_keys, KEY_VALUE_HEADS * HEAD_SIZE)
            grad_keys_all = lax.dynamic_update_slice_in_dim(grad_keys_all, key_part, row_start, 0)
            grad_values_all = lax.dynamic_update_slice_in_dim(
                grad_values_all, value_part, row_start, 0
            )
            return (grad_query_acc, grad_keys_all, grad_values_all)

        start_back = (
            jnp.zeros(
                (rows_per_shard, KEY_VALUE_HEADS, head_repeat_factor, HEAD_SIZE), jnp.float32
            ),
            jnp.zeros((rows_per_group, KEY_VALUE_HEADS * HEAD_SIZE), jnp.float32),
            jnp.zeros((rows_per_group, KEY_VALUE_HEADS * HEAD_SIZE), jnp.float32),
        )
        grad_query_acc, grad_keys_all, grad_values_all = lax.fori_loop(
            0, count_of_blocks, pass_back, start_back
        )
        own_key_gradient, grad_values_own = (
            lax.psum_scatter(
                grad_keys_all.astype(jnp.bfloat16), "seq", scatter_dimension=0, tiled=True
            ).astype(jnp.float32),
            lax.psum_scatter(
                grad_values_all.astype(jnp.bfloat16), "seq", scatter_dimension=0, tiled=True
            ).astype(jnp.float32),
        )
        grad_query_pre = (
            inverse_rotary(
                grad_query_acc.reshape(rows_per_shard, QUERY_HEADS, HEAD_SIZE) * scale,
                cosine_lookup,
                sine_lookup,
            )
            .astype(jnp.bfloat16)
            .reshape(rows_per_shard, QUERY_HEADS * HEAD_SIZE)
        )
        grad_key_pre = (
            inverse_rotary(
                own_key_gradient.reshape(rows_per_shard, KEY_VALUE_HEADS, HEAD_SIZE),
                cosine_lookup,
                sine_lookup,
            )
            .astype(jnp.bfloat16)
            .reshape(rows_per_shard, KEY_VALUE_HEADS * HEAD_SIZE)
        )
        grad_value_pre = grad_values_own.astype(jnp.bfloat16)
        grad_query_w = inner_rows(act_one, grad_query_pre)
        grad_key_w = inner_rows(act_one, grad_key_pre)
        grad_value_w = inner_rows(act_one, grad_value_pre)
        grad_act_one = (
            times_transpose(grad_query_pre, query_full)
            + times_transpose(grad_key_pre, key_full)
            + times_transpose(grad_value_pre, value_full)
        )
        grad_rows_norm, grad_gain_attn = norm_back(grad_act_one, rows_in, inverse_one, gain_attn)
        grad_input_list.append(grad_hidden + grad_rows_norm)
        attn_grads = (grad_query_w, grad_key_w, grad_value_w, grad_out, grad_gain_attn)
        reduced = reduce_attention(attn_grads) + reduce_mlp(mlp_grads)
        owned = reduced if owned is None else tuple(jax.tree.map(jnp.add, owned, reduced))
    outputs = jnp.stack(output_list)[:, None]
    grad_inputs = jnp.stack(grad_input_list)[:, None]
    return (
        outputs,
        grad_inputs,
        owned[0],
        owned[1],
        owned[2],
        owned[3],
        owned[4],
        owned[5],
        owned[6],
        owned[7],
        owned[8],
    )


def solution(mesh):
    return jax.shard_map(
        on_device,
        mesh=mesh,
        in_specs=(
            P(None, "grp", "seq", None),
            P(None, "grp", None),
            P(("grp", "seq"), None),
            P(("grp", "seq"), None),
            P(("grp", "seq"), None),
            P(None, ("grp", "seq")),
            P(("grp", "seq")),
            P(("grp", "seq"), None),
            P(("grp", "seq"), None),
            P(("grp", "seq"), None),
            P(("grp", "seq")),
            P(None, "grp", "seq", None),
        ),
        out_specs=(
            P(None, "grp", "seq", None),
            P(None, "grp", "seq", None),
            P(("grp", "seq"), None),
            P(("grp", "seq"), None),
            P(("grp", "seq"), None),
            P(None, ("grp", "seq")),
            P(("grp", "seq")),
            P(("grp", "seq"), None),
            P(("grp", "seq"), None),
            P(("grp", "seq"), None),
            P(("grp", "seq")),
        ),
        check_vma=False,
    )
```

profile of v0, /device:TPU:0, one launch (start us, length us, event | category | flops | bytes accessed | tf_op | source)
XLA Modules:
  0.0 2016.9 jit_solution(3304292125862023898)
XLA Ops:
  16.1 42.2 %all-reduce.5 = (bf16[1536]{0:T(1024)(128)(2,1)S(1)}, bf16[1536]{0:T(1024)(128)(2,1)S(1)}) all-reduce(bf16[1536]{0:T(1024)(128)(2,1)S(1)} %dynamic-update-slice, bf16[1536]{0:T(1024)(128)(2,1)S(1)} %dynamic-update-slice.1), channel_id=1, replica_groups=mesh['grp'=8,'seq'=4] {'grp','seq'}, use_global_device_ids=true, to_apply=%add | all-reduce | flops 3072 | bytes 12288
  82.9 46.8 %all-gather.8.cloned.1.call-done = bf16[1536,768]{1,0:T(8,128)(2,1)} async-done(((bf16[48,768]{1,0:T(8,128)(2,1)}), bf16[1536,768]{1,0:T(8,128)(2,1)}) %all-gather.8.cloned.1.call-update) | async-done | bytes 2359312 | tf_op jit(solution)/shard_map/all_gather | solution.py:152
  148.0 9.6 all_gather.50
  157.7 9.2 all_gather.41
  166.8 28.6 %all-gather.10.cloned.1.call-done = bf16[1536,1536]{1,0:T(8,128)(2,1)} async-done(((bf16[48,1536]{1,0:T(8,128)(2,1)}), bf16[1536,1536]{1,0:T(8,128)(2,1)}) %all-gather.10.cloned.1.call-update) | async-done | bytes 4718608 | tf_op jit(solution)/shard_map/all_gather | solution.py:151
  217.5 13.5 while.91
  248.8 11.3 all-gather.14.cloned.1.call-done
  268.2 88.1 %all-gather.16.cloned.1.call-done = bf16[1536,4096]{1,0:T(8,128)(2,1)} async-done(((bf16[48,4096]{1,0:T(8,128)(2,1)}), bf16[1536,4096]{1,0:T(8,128)(2,1)}) %all-gather.16.cloned.1.call-update) | async-done | bytes 12582928 | tf_op jit(solution)/shard_map/all_gather | solution.py:158
  362.8 90.2 %all-gather.18.cloned.1.call-done = bf16[1536,4096]{1,0:T(8,128)(2,1)} async-done(((bf16[48,4096]{1,0:T(8,128)(2,1)}), bf16[1536,4096]{1,0:T(8,128)(2,1)}) %all-gather.18.cloned.1.call-update) | async-done | bytes 12582928 | tf_op jit(solution)/shard_map/all_gather | solution.py:159
  460.7 89.0 %all-gather.20.cloned.1.call-done = bf16[4096,1536]{1,0:T(8,128)(2,1)} async-done(((bf16[128,1536]{1,0:T(8,128)(2,1)}), bf16[4096,1536]{1,0:T(8,128)(2,1)}) %all-gather.20.cloned.1.call-update) | async-done | bytes 12582928 | tf_op jit(solution)/shard_map/all_gather | solution.py:160
  549.6 10.8 multiply_convert_fusion.2
  560.4 10.1 fusion.119
  570.6 11.8 multiply_reduce_fusion.1
  593.2 9.9 multiply_convert_fusion
  603.2 9.6 fusion.121
  612.9 9.9 multiply_reduce_fusion
  678.1 22.4 %reduce-scatter.34.cloned.1.call-done = bf16[128,768]{1,0:T(8,128)(2,1)} async-done(((bf16[512,768]{1,0:T(8,128)(2,1)}), bf16[128,768]{1,0:T(8,128)(2,1)}) %reduce-scatter.34.cloned.1.call-update) | async-done | bytes 196624
  709.1 17.0 reduce-scatter.36.cloned.1.call-done
  730.0 22.4 %reduce-scatter.40.cloned.1.call-done = bf16[128,768]{1,0:T(8,128)(2,1)} async-done(((bf16[512,768]{1,0:T(8,128)(2,1)}), bf16[128,768]{1,0:T(8,128)(2,1)}) %reduce-scatter.40.cloned.1.call-update) | async-done | bytes 196624
  777.2 10.4 fusion.123
  787.7 17.5 convolution_add_fusion.2
  806.3 10.1 fusion.124
  816.5 17.0 convolution_add_fusion.1
  834.7 11.4 fusion.63
  846.1 17.2 convolution_add_fusion
  886.9 39.7 %all-reduce.4 = (f32[1536]{0:T(1024)S(1)}, f32[1536]{0:T(1024)S(1)}) all-reduce(f32[1536]{0:T(1024)S(1)} %add.422, f32[1536]{0:T(1024)S(1)} %add.426), channel_id=19, replica_groups=mesh['grp'=8,'seq'=4] {'grp','seq'}, use_global_device_ids=true, to_apply=%region_45.46.clone | all-reduce | flops 3072 | bytes 24576
  930.6 48.6 %reduce-scatter.24.cloned.1.call-done = f32[48,768]{1,0:T(8,128)} async-done(((f32[1536,768]{1,0:T(8,128)}), f32[48,768]{1,0:T(8,128)}) %reduce-scatter.24.cloned.1.call-update) | async-done | bytes 147472 | tf_op jit(solution)/shard_map/reduce_scatter | solution.py:99
  979.2 141.5 %reduce-scatter.20.cloned.1.call-done = f32[48,1536]{1,0:T(8,128)} async-done(((f32[1536,1536]{1,0:T(8,128)}), f32[48,1536]{1,0:T(8,128)}) %reduce-scatter.20.cloned.1.call-update) | async-done | bytes 294928 | tf_op jit(solution)/shard_map/reduce_scatter | solution.py:97
  1120.7 141.5 %reduce-scatter.26.cloned.1.call-done = f32[1536,48]{0,1:T(8,128)} async-done(((f32[1536,1536]{0,1:T(8,128)}), f32[1536,48]{0,1:T(8,128)}) %reduce-scatter.26.cloned.1.call-update) | async-done | bytes 294928 | tf_op jit(solution)/shard_map/reduce_scatter | solution.py:100
  1262.2 248.8 %reduce-scatter.28.cloned.1.call-done = f32[48,4096]{1,0:T(8,128)} async-done(((f32[1536,4096]{1,0:T(8,128)}), f32[48,4096]{1,0:T(8,128)}) %reduce-scatter.28.cloned.1.call-update) | async-done | bytes 786448 | tf_op jit(solution)/shard_map/reduce_scatter | solution.py:109
  1511.0 249.4 %reduce-scatter.30.cloned.1.call-done = f32[48,4096]{1,0:T(8,128)} async-done(((f32[1536,4096]{1,0:T(8,128)}), f32[48,4096]{1,0:T(8,128)}) %reduce-scatter.30.cloned.1.call-update) | async-done | bytes 786448 | tf_op jit(solution)/shard_map/reduce_scatter | solution.py:110
  1760.4 249.4 %reduce-scatter.32.cloned.1.call-done = f32[128,1536]{1,0:T(8,128)} async-done(((f32[4096,1536]{1,0:T(8,128)}), f32[128,1536]{1,0:T(8,128)}) %reduce-scatter.32.cloned.1.call-update) | async-done | bytes 786448 | tf_op jit(solution)/shard_map/reduce_scatter | solution.py:111
  (465 shorter events, 255.4 us)
Async XLA Ops:
  7.2 63.6 %all-gather.12.cloned.1.call-start = ((), (), s32[]{:S(2)}) async-start(), calls=%async_computation.13 | async-start | bytes 2433024 | tf_op jit(solution)/shard_map/all_gather | solution.py:153
  7.9 121.8 %all-gather.8.cloned.1.call-start = ((), (), s32[]{:S(2)}) async-start(), calls=%async_computation.11 | async-start | bytes 2433024 | tf_op jit(solution)/shard_map/all_gather | solution.py:152
  8.7 186.8 %all-gather.10.cloned.1.call-start = ((), (), s32[]{:S(2)}) async-start(), calls=%async_computation.12 | async-start | bytes 4866048 | tf_op jit(solution)/shard_map/all_gather | solution.py:151
  9.4 250.7 %all-gather.14.cloned.1.call-start = ((), (), s32[]{:S(2)}) async-start(), calls=%async_computation.14 | async-start | bytes 4866048 | tf_op jit(solution)/shard_map/all_gather | solution.py:154
  10.0 346.4 %all-gather.16.cloned.1.call-start = ((), (), s32[]{:S(2)}) async-start(), calls=%async_computation.15 | async-start | bytes 12976128 | tf_op jit(solution)/shard_map/all_gather | solution.py:158
  10.6 442.4 %all-gather.18.cloned.1.call-start = ((), (), s32[]{:S(2)}) async-start(), calls=%async_computation.16 | async-start | bytes 12976128 | tf_op jit(solution)/shard_map/all_gather | solution.py:159
  11.1 538.5 %all-gather.20.cloned.1.call-start = ((), (), s32[]{:S(2)}) async-start(), calls=%async_computation.17 | async-start | bytes 12976128 | tf_op jit(solution)/shard_map/all_gather | solution.py:160
  11.9 662.7 %reduce-scatter.38.cloned.1.call-start = ((), (), s32[]{:S(2)}) async-start(), calls=%async_computation.27 | async-start | bytes 983040
  13.8 47.6 %copy-start.77 = (s32[512]{0:T(512)}, s32[512]{0:T(512)S(1)}, u32[]{:S(2)}) copy-start(s32[512]{0:T(512)S(1)} %get-tuple-element.1600) | copy-start | bytes 6148
  13.8 47.6 %copy-start.79 = (s32[512]{0:T(512)}, s32[512]{0:T(512)S(1)}, u32[]{:S(2)}) copy-start(s32[512]{0:T(512)S(1)} %get-tuple-element.1549) | copy-start | bytes 6148
  13.9 118.7 %copy-start.108 = (s32[128]{0:T(128)}, s32[128]{0:T(128)S(1)}, u32[]{:S(2)}) copy-start(s32[128]{0:T(128)S(1)} %dynamic_slice.17) | copy-start | bytes 1540
  14.1 118.5 %copy-start.106 = (s32[128]{0:T(128)}, s32[128]{0:T(128)S(1)}, u32[]{:S(2)}) copy-start(s32[128]{0:T(128)S(1)} %dynamic_slice.11) | copy-start | bytes 1540
  58.3 704.5 %copy-start.64 = (f32[1536]{0:T(1024)}, f32[1536]{0:T(1024)S(1)}, u32[]{:S(2)}) copy-start(f32[1536]{0:T(1024)S(1)} %convert_element_type.265) | copy-start | bytes 18436
  60.8 71.8 %copy-start.91 = (f32[128]{0:T(128)}, f32[128]{0:T(128)S(1)}, u32[]{:S(2)}) copy-start(f32[128]{0:T(128)S(1)} %get-tuple-element.1262) | copy-start | bytes 1540
  60.8 85.4 %copy-start.98 = (f32[128]{0:T(128)}, f32[128]{0:T(128)S(1)}, u32[]{:S(2)}) copy-start(f32[128]{0:T(128)S(1)} %get-tuple-element.1239) | copy-start | bytes 1540
  61.1 149.5 %copy-start.66 = (pred[128,512]{0,1:T(8,128)(4,1)}, pred[128,512]{0,1:T(8,128)(4,1)S(1)}, u32[]{:S(2)}) copy-start(pred[128,512]{0,1:T(8,128)(4,1)S(1)} %compare_and_fusion.2) | copy-start | bytes 196612
  61.7 85.3 %copy-start.74 = (f32[128,48]{0,1:T(8,128)}, f32[128,48]{0,1:T(8,128)S(1)}, u32[]{:S(2)}) copy-start(f32[128,48]{0,1:T(8,128)S(1)} %get-tuple-element.1245) | copy-start | bytes 73732
  61.7 144.3 %copy-start.72 = (f32[128,48]{0,1:T(8,128)}, f32[128,48]{0,1:T(8,128)S(1)}, u32[]{:S(2)}) copy-start(f32[128,48]{0,1:T(8,128)S(1)} %get-tuple-element.1244) | copy-start | bytes 73732
  61.7 174.5 %copy-start.70 = (f32[128,48]{0,1:T(8,128)}, f32[128,48]{0,1:T(8,128)S(1)}, u32[]{:S(2)}) copy-start(f32[128,48]{0,1:T(8,128)S(1)} %get-tuple-element.1229) | copy-start | bytes 73732
  73.1 59.6 %copy-start.1 = (bf16[2,1,128,1536]{3,2,1,0:T(8,128)(2,1)S(1)}, bf16[2,1,128,1536]{3,2,1,0:T(8,128)(2,1)}, u32[]{:S(2)}) copy-start(bf16[2,1,128,1536]{3,2,1,0:T(8,128)(2,1)} %param.24) | copy-start | bytes 2359300
  268.2 184.7 %copy-start.14 = (bf16[128,1536]{1,0:T(8,128)(2,1)}, bf16[128,1536]{1,0:T(8,128)(2,1)S(1)}, u32[]{:S(2)}) copy-start(bf16[128,1536]{1,0:T(8,128)(2,1)S(1)} %multiply_convert_fusion.7) | copy-start | bytes 1179652
  362.8 186.9 %copy-start.56 = (bf16[2,1,128,1536]{3,2,1,0:T(8,128)(2,1)S(1)}, bf16[2,1,128,1536]{3,2,1,0:T(8,128)(2,1)}, u32[]{:S(2)}) copy-start(bf16[2,1,128,1536]{3,2,1,0:T(8,128)(2,1)} %param.35) | copy-start | bytes 2359300
  652.7 47.7 %reduce-scatter.34.cloned.1.call-start = ((), (), s32[]{:S(2)}) async-start(), calls=%async_computation.25 | async-start | bytes 983040
  667.5 58.6 %reduce-scatter.36.cloned.1.call-start = ((), (), s32[]{:S(2)}) async-start(), calls=%async_computation.26 | async-start | bytes 983040
  669.9 82.5 %reduce-scatter.40.cloned.1.call-start = ((), (), s32[]{:S(2)}) async-start(), calls=%async_computation.28 | async-start | bytes 983040
  672.3 258.4 %reduce-scatter.22.cloned.1.call-start = ((), (), s32[]{:S(2)}) async-start(), calls=%async_computation.19 | async-start | bytes 4866048 | tf_op jit(solution)/shard_map/reduce_scatter | solution.py:98
  709.0 270.2 %reduce-scatter.24.cloned.1.call-start = ((), (), s32[]{:S(2)}) async-start(), calls=%async_computation.20 | async-start | bytes 4866048 | tf_op jit(solution)/shard_map/reduce_scatter | solution.py:99
  757.9 362.8 %reduce-scatter.20.cloned.1.call-start = ((), (), s32[]{:S(2)}) async-start(), calls=%async_computation.18 | async-start | bytes 9732096 | tf_op jit(solution)/shard_map/reduce_scatter | solution.py:97
  768.1 494.0 %reduce-scatter.26.cloned.1.call-start = ((), (), s32[]{:S(2)}) async-start(), calls=%async_computation.21 | async-start | bytes 9732096 | tf_op jit(solution)/shard_map/reduce_scatter | solution.py:100
  775.9 735.1 %reduce-scatter.28.cloned.1.call-start = ((), (), s32[]{:S(2)}) async-start(), calls=%async_computation.22 | async-start | bytes 25952256 | tf_op jit(solution)/shard_map/reduce_scatter | solution.py:109
  805.1 955.2 %reduce-scatter.30.cloned.1.call-start = ((), (), s32[]{:S(2)}) async-start(), calls=%async_computation.23 | async-start | bytes 25952256 | tf_op jit(solution)/shard_map/reduce_scatter | solution.py:110
  833.5 1176.3 %reduce-scatter.32.cloned.1.call-start = ((), (), s32[]{:S(2)}) async-start(), calls=%async_computation.24 | async-start | bytes 25952256 | tf_op jit(solution)/shard_map/reduce_scatter | solution.py:111
  (113 other events, 1098.9 us)
Sparse Core Ops, SparseCore 0:
  10.9 59.7 all-gather.11
  73.6 56.0 all-gather.7
  132.7 62.7 all-gather.9
  198.2 61.8 all-gather.13
  262.8 93.4 all-gather.15
  359.1 93.7 all-gather.17
  455.8 93.7 all-gather.19
  652.8 21.7 reduce-scatter.37
  677.2 23.2 reduce-scatter.33
  702.8 23.1 reduce-scatter.35
  729.2 23.1 reduce-scatter.39
  758.3 107.8 reduce-scatter.21
  872.2 106.9 reduce-scatter.23
  985.5 135.1 reduce-scatter.19
  1127.0 135.0 reduce-scatter.25
  1269.0 241.9 reduce-scatter.27
  1517.8 242.5 reduce-scatter.29
  1767.2 242.5 reduce-scatter.31
where the time goes:
time: 2030 us; the launch traced here: 2020 us
  waiting for transfers between devices  1510 us (74%)
  matrix products  275 us (14%)
  blocking collectives  118 us (6%)
  local copies, waits for them, and re-layouts  58.7 us (3%)
  other arithmetic  22.7 us (1%)
    reduce_scatter x1, waiting for transfers between devices, reduce_mlp(): lax.psum_scatter(grad_list[2], ('grp', 'seq'), scatter_dimension=0, tiled...  249 us
    reduce_scatter x1, waiting for transfers between devices, reduce_mlp(): lax.psum_scatter(grad_list[1], ('grp', 'seq'), scatter_dimension=0, tiled...  249 us
    reduce_scatter x1, waiting for transfers between devices, reduce_mlp(): lax.psum_scatter(grad_list[0], ('grp', 'seq'), scatter_dimension=0, tiled...  249 us
    reduce_scatter x1, waiting for transfers between devices, reduce_attention(): lax.psum_scatter(grad_list[0], ('grp', 'seq'), scatter_dimension=0, tiled...  141 us
    reduce_scatter x1, waiting for transfers between devices, reduce_attention(): lax.psum_scatter(grad_list[3], ('grp', 'seq'), scatter_dimension=1, tiled...  141 us
    dot_general x14, matrix products, inner_rows(): lax.dot_general(left, right, (((0,), (0,)), ((), ())), preferred_element_...  110 us
    all_gather x1, waiting for transfers between devices, on_device(): lax.all_gather(w_up, ('grp', 'seq'), axis=0, tiled=True)  90.2 us
    all_gather x1, waiting for transfers between devices, on_device(): lax.all_gather(w_down, ('grp', 'seq'), axis=0, tiled=True)  89 us
  transfers between devices with their start and end apart: 18, of which 17 were waited for; matrix products, arithmetic and copies ran while one was open for 12% of the time, Pallas kernels for 0%

commit v1 on v0

v1 whole, which is shorter than its diff:
```python
import jax
import jax.numpy as jnp
from jax import lax
from jax.sharding import Mesh
from jax.sharding import PartitionSpec as P

QUERY_HEADS = 16
KEY_VALUE_HEADS = 8
HEAD_SIZE = 96
CONT_MEAN = 224

EPSILON = 1e-05
ROPE_BASE = 100000.0
MASK_FILL = -1e30
CHIPS = ("grp", "row")
F32 = jnp.float32
BF16 = jnp.bfloat16


def layout(lengths, row_ids, prompt_rows):
    cont_ends = prompt_rows + jnp.cumsum(lengths)
    cont_starts = cont_ends - lengths
    member = (
        (row_ids[:, None] >= cont_starts[None, :]) & (row_ids[:, None] < cont_ends[None, :])
    ).astype(jnp.int32)
    labels = jnp.arange(1, lengths.shape[0] + 1, dtype=jnp.int32)
    segment = jnp.sum(member * labels[None, :], axis=1)
    offsets = jnp.sum(member * cont_starts[None, :], axis=1)
    position = jnp.where(segment > 0, prompt_rows + row_ids - offsets, row_ids)
    return (segment, position)


def rotation(position):
    half_dim = HEAD_SIZE // 2
    frequency = ROPE_BASE ** (-2.0 * jnp.arange(half_dim, dtype=F32) / HEAD_SIZE)
    angles = position.astype(F32)[..., None] * frequency
    return (jnp.cos(angles)[..., None, :], jnp.sin(angles)[..., None, :])


def rotate(head_values, cosine, sine):
    half_dim = HEAD_SIZE // 2
    first, second = head_values[..., :half_dim], head_values[..., half_dim:]
    return jnp.concatenate(
        [first * cosine - second * sine, second * cosine + first * sine], axis=-1
    )


def dot(left, right, left_dim, right_dim):
    return lax.dot_general(
        left, right, (((left_dim,), (right_dim,)), ((), ())), preferred_element_type=F32
    )


def swap(value):
    return lax.ppermute(value, "core", [(0, 1), (1, 0)])


def take_half(value, which):
    half = value.shape[1] // 2
    return lax.dynamic_slice_in_dim(value, which * half, half, 1)


def on_device(
    inputs,
    cont_lengths,
    w_query,
    key_projection,
    value_projection,
    w_out,
    attn_gain,
    w_gate,
    w_up,
    w_down,
    mlp_gain,
    cotangent,
):
    micros, _, rows_own, width = inputs.shape
    n_row = lax.axis_size("row")
    chips = lax.axis_size("grp") * n_row
    core = lax.axis_index("core")
    chip_row = lax.axis_index("row")
    rows_chip = 2 * rows_own
    rows_group = rows_chip * n_row
    rows = micros * rows_chip
    prompt_rows = rows_group - CONT_MEAN * cont_lengths.shape[2]
    repeat = QUERY_HEADS // KEY_VALUE_HEADS
    kv_heads = KEY_VALUE_HEADS // 2
    q_heads = QUERY_HEADS // 2
    q_cols, kv_cols = q_heads * HEAD_SIZE, kv_heads * HEAD_SIZE
    scale = HEAD_SIZE ** (-0.5)
    feats = w_query.shape[0]
    hidden_own = w_down.shape[0]
    ff_half = hidden_own * chips

    gain_one = attn_gain.astype(F32)[:, None]
    gain_two = mlp_gain.astype(F32)[:, None]

    def ff_part(value, which):
        parts = value.reshape(feats, chips, 2, hidden_own)
        return lax.dynamic_index_in_dim(parts, which, 2, keepdims=False).reshape(feats, ff_half)

    def scaled(value, gain):
        return (value.astype(F32) * gain).astype(BF16)

    def in_order(own, other):
        return jnp.where(
            core == 0, jnp.concatenate([own, other]), jnp.concatenate([other, own])
        )

    query_scaled, key_scaled, value_scaled = (
        scaled(w, gain_one) for w in (w_query, key_projection, value_projection)
    )
    out_turned = w_out.T

    def attn_part(which):
        return jnp.concatenate(
            [take_half(w, which) for w in (query_scaled, key_scaled, value_scaled, out_turned)],
            axis=1,
        )

    def gather(block):
        return lax.all_gather(block, CHIPS, axis=0, tiled=True)

    attn_block = in_order(attn_part(core), swap(attn_part(1 - core)))
    qkv_cols = q_cols + 2 * kv_cols
    qkv_full = gather(attn_block[:, :qkv_cols])
    out_full = gather(attn_block[:, qkv_cols:])

    gate_scaled, up_scaled = scaled(w_gate, gain_two), scaled(w_up, gain_two)

    def mlp_part(which):
        return jnp.concatenate([ff_part(gate_scaled, which), ff_part(up_scaled, which)], axis=1)

    mlp_block = in_order(mlp_part(core), swap(mlp_part(1 - core)))
    gate_full = gather(mlp_block[:, :ff_half])
    up_full = gather(mlp_block[:, ff_half:])
    down_full = gather(w_down)

    def both(own):
        return jnp.concatenate([own, swap(own)], axis=1)

    def add_partner(part, back=None):
        low = part.reshape(micros, rows_chip, width).astype(BF16)
        mine = swap(low[:, rows_own:])
        theirs = swap(low[:, :rows_own])
        return part + jnp.concatenate([mine, theirs], axis=1).reshape(rows, width).astype(F32)

    def own_sum(part):
        parts = part.reshape(micros, rows_chip, width)
        return parts[:, :rows_own] + swap(parts[:, rows_own:].astype(BF16)).astype(F32)

    def own_rows(value):
        return value.reshape(micros, rows_chip, -1)[:, :rows_own]

    x_pair = both(inputs[:, 0])
    cot_pair = both(cotangent[:, 0]).reshape(rows, width)
    xf = x_pair.reshape(rows, width).astype(F32)

    if n_row == 2:
        row_order = jnp.stack([chip_row, 1 - chip_row])
    else:
        row_order = jnp.arange(n_row)
    halves = jnp.stack([core, 1 - core])
    chip_ids = (halves[:, None] * rows_own + jnp.arange(rows_own)[None, :]).reshape(-1)
    query_ids = chip_row * rows_chip + chip_ids
    key_ids = (row_order[:, None] * rows_chip + chip_ids[None, :]).reshape(-1)
    segments = [layout(cont_lengths[m, 0], query_ids, prompt_rows) for m in range(micros)]
    key_segments = [layout(cont_lengths[m, 0], key_ids, prompt_rows) for m in range(micros)]
    segment_q, position_q = (jnp.stack(v) for v in zip(*segments))
    segment_k, position_k = (jnp.stack(v) for v in zip(*key_segments))
    visible = (
        ((segment_k[:, None, :] == 0) | (segment_k[:, None, :] == segment_q[:, :, None]))
        & (position_k[:, None, :] <= position_q[:, :, None])
    )[:, None, None]
    cosine, sine = rotation(position_q)

    inverse_one = lax.rsqrt(jnp.mean(xf * xf, axis=-1, keepdims=True) + EPSILON)
    act_one = (xf * inverse_one).astype(BF16)
    qkv = dot(act_one, qkv_full, 1, 0).reshape(micros, rows_chip, qkv_cols)
    queries = (
        rotate(
            qkv[..., :q_cols].reshape(micros, rows_chip, q_heads, HEAD_SIZE), cosine, sine
        )
        * scale
    ).astype(BF16)
    keys_own = (
        rotate(
            qkv[..., q_cols : q_cols + kv_cols].reshape(micros, rows_chip, kv_heads, HEAD_SIZE),
            cosine,
            sine,
        )
        .astype(BF16)
        .reshape(micros, rows_chip, kv_cols)
    )
    values_own = qkv[..., q_cols + kv_cols :].astype(BF16)
    key_value = jnp.concatenate([keys_own, values_own], axis=2)
    flip = [(0, 1), (1, 0)]
    if n_row == 2:
        key_value = jnp.concatenate([key_value, lax.ppermute(key_value, "row", flip)], axis=1)
    else:
        key_value = lax.all_gather(key_value, "row", axis=1, tiled=True)
    keys_all = key_value[..., :kv_cols].reshape(micros, rows_group, kv_heads, HEAD_SIZE)
    values_all = key_value[..., kv_cols:].reshape(micros, rows_group, kv_heads, HEAD_SIZE)
    grouped = queries.reshape(micros, rows_chip, kv_heads, repeat, HEAD_SIZE)

    scores = jnp.einsum("mrgjd,mkgd->mgjrk", grouped, keys_all, preferred_element_type=F32)
    scores = jnp.where(visible, scores, MASK_FILL)
    top = jnp.max(scores, axis=-1, keepdims=True)
    weights = jnp.exp(scores - top)
    probs = weights / jnp.sum(weights, axis=-1, keepdims=True)
    probs_low = probs.astype(BF16)
    attn = jnp.einsum("mgjrk,mkgd->mrgjd", probs_low, values_all, preferred_element_type=F32)
    attn_low = attn.reshape(rows, q_cols).astype(BF16)

    hidden = xf + add_partner(dot(attn_low, out_full, 1, 1))
    inverse_two = lax.rsqrt(jnp.mean(hidden * hidden, axis=-1, keepdims=True) + EPSILON)
    act_two = (hidden * inverse_two).astype(BF16)
    gate_pre = dot(act_two, gate_full, 1, 0)
    up_pre = dot(act_two, up_full, 1, 0)
    sigmoid_gate = jax.nn.sigmoid(gate_pre)
    silu_gate = gate_pre * sigmoid_gate
    mixed = (silu_gate * up_pre).astype(BF16)

    def scatter(grad):
        return lax.psum_scatter(grad.astype(BF16), CHIPS, scatter_dimension=0, tiled=True)

    grad_down = scatter(dot(mixed, cot_pair, 0, 0)).astype(F32)
    outputs = (own_rows(hidden) + own_sum(dot(mixed, down_full, 1, 0))).astype(BF16)
    grad_mixed = dot(cot_pair, down_full, 1, 1)
    grad_gate_pre = (
        grad_mixed * up_pre * sigmoid_gate * (1.0 + gate_pre * (1.0 - sigmoid_gate))
    ).astype(BF16)
    grad_up_pre = (grad_mixed * silu_gate).astype(BF16)
    grad_gate_half = scatter(dot(act_two, grad_gate_pre, 0, 0))
    grad_up_half = scatter(dot(act_two, grad_up_pre, 0, 0))
    back_two = add_partner(dot(grad_gate_pre, gate_full, 1, 1) + dot(grad_up_pre, up_full, 1, 1))
    grad_hidden = (
        cot_pair.astype(F32)
        + inverse_two * back_two
        - hidden * inverse_two**3 * jnp.mean(back_two * hidden, axis=-1, keepdims=True)
    )
    hidden_low = grad_hidden.astype(BF16)
    grad_out_half = scatter(dot(hidden_low, attn_low, 0, 0))
    attn_grad = (
        dot(hidden_low, out_full, 1, 0)
        .astype(BF16)
        .reshape(micros, rows_chip, kv_heads, repeat, HEAD_SIZE)
    )
    grad_probs = jnp.einsum("mrgjd,mkgd->mgjrk", attn_grad, values_all, preferred_element_type=F32)
    delta = jnp.sum(probs * grad_probs, axis=-1, keepdims=True)
    grad_scores = (probs * (grad_probs - delta)).astype(BF16)
    grad_queries = jnp.einsum(
        "mgjrk,mkgd->mrgjd", grad_scores, keys_all, preferred_element_type=F32
    )
    grad_keys = jnp.einsum("mgjrk,mrgjd->mkgd", grad_scores, grouped, preferred_element_type=F32)
    grad_values = jnp.einsum("mgjrk,mrgjd->mkgd", probs_low, attn_grad, preferred_element_type=F32)
    grad_kv = jnp.concatenate(
        [
            grad_keys.reshape(micros, rows_group, kv_cols),
            grad_values.reshape(micros, rows_group, kv_cols),
        ],
        axis=2,
    )
    if n_row == 2:
        grad_kv = grad_kv[:, :rows_chip] + lax.ppermute(
            grad_kv[:, rows_chip:].astype(BF16), "row", flip
        ).astype(F32)
    else:
        grad_kv = lax.psum_scatter(
            grad_kv.astype(BF16), "row", scatter_dimension=1, tiled=True
        ).astype(F32)
    grad_query_pre = rotate(
        grad_queries.reshape(micros, rows_chip, q_heads, HEAD_SIZE) * scale, cosine, -sine
    ).reshape(micros, rows_chip, q_cols)
    grad_key_pre = rotate(
        grad_kv[..., :kv_cols].reshape(micros, rows_chip, kv_heads, HEAD_SIZE), cosine, -sine
    ).reshape(micros, rows_chip, kv_cols)
    grad_qkv_pre = (
        jnp.concatenate([grad_query_pre, grad_key_pre, grad_kv[..., kv_cols:]], axis=2)
        .astype(BF16)
        .reshape(rows, qkv_cols)
    )
    grad_qkv_half = scatter(dot(act_one, grad_qkv_pre, 0, 0))
    back_one = own_sum(dot(grad_qkv_pre, qkv_full, 1, 1))
    x_own = inputs[:, 0].astype(F32)
    inverse_own = own_rows(inverse_one)
    grad_inputs = (
        own_rows(grad_hidden)
        + inverse_own * back_one
        - x_own * inverse_own**3 * jnp.mean(back_one * x_own, axis=-1, keepdims=True)
    )

    def regroup(half):
        own = lax.dynamic_slice_in_dim(half, core * feats, feats, 0)
        other = swap(lax.dynamic_slice_in_dim(half, (1 - core) * feats, feats, 0))
        return own.astype(F32), other.astype(F32)

    def join_columns(own, other):
        return jnp.where(
            core == 0,
            jnp.concatenate([own, other], axis=1),
            jnp.concatenate([other, own], axis=1),
        )

    def join_ff(pair):
        own, other = (part.reshape(feats, chips, 1, hidden_own) for part in pair)
        return jnp.where(
            core == 0,
            jnp.concatenate([own, other], axis=2),
            jnp.concatenate([other, own], axis=2),
        ).reshape(feats, 2 * ff_half)

    bare_gate, bare_up = join_ff(regroup(grad_gate_half)), join_ff(regroup(grad_up_half))
    grad_mlp_gain = jnp.sum(
        bare_gate * w_gate.astype(F32) + bare_up * w_up.astype(F32), axis=1
    )
    own, other = regroup(grad_qkv_half)
    bare_query, bare_key, bare_value = (
        join_columns(own[:, a:b], other[:, a:b])
        for a, b in ((0, q_cols), (q_cols, q_cols + kv_cols), (q_cols + kv_cols, qkv_cols))
    )
    grad_attn_gain = jnp.sum(bare_query * w_query.astype(F32), axis=1) + jnp.sum(
        bare_key * key_projection.astype(F32) + bare_value * value_projection.astype(F32), axis=1
    )
    grad_out = join_columns(*regroup(grad_out_half)).T
    return (
        outputs[:, None],
        grad_inputs[:, None],
        bare_query * gain_one,
        bare_key * gain_one,
        bare_value * gain_one,
        grad_out,
        grad_attn_gain,
        bare_gate * gain_two,
        bare_up * gain_two,
        grad_down,
        grad_mlp_gain,
    )


def solution(mesh):
    grp, seq = mesh.shape["grp"], mesh.shape["seq"]
    split = Mesh(mesh.devices.reshape(grp, seq // 2, 2), ("grp", "row", "core"))
    every = ("grp", "row", "core")
    rows = P(None, "grp", ("row", "core"), None)
    sharded, column = P(every, None), P(None, every)
    return jax.shard_map(
        on_device,
        mesh=split,
        in_specs=(
            rows,
            P(None, "grp", None),
            sharded,
            sharded,
            sharded,
            column,
            P(every),
            sharded,
            sharded,
            sharded,
            P(every),
            rows,
        ),
        out_specs=(
            rows,
            rows,
            sharded,
            sharded,
            sharded,
            column,
            P(every),
            sharded,
            sharded,
            sharded,
            P(every),
        ),
        check_vma=False,
    )
```

time: 2030 us -> 1250 us (0.62)
  waiting for transfers between devices: 1510 us -> 993 us
  matrix products: 275 us -> 122 us
  blocking collectives: 118 us -> 0 us
  other arithmetic: 22.7 us -> 48.6 us
    reduce_scatter x7 -> x5, waiting for transfers between devices: 1080 us -> 612 us  [scatter(): lax.psum_scatter(grad.astype(BF16), CHIPS, scatter_dimension=0, tiled=True)]
    dot_general x56 -> x20, matrix products: 275 us -> 117 us  [the longest x15 95.6 us: dot(): lax.dot_general(left, right, (((left_dim,), (right_dim,)), ((), ())), pre...]
    unnamed x2 -> x0, blocking collectives: 81.9 us -> none
    unnamed x22 -> x10, waiting for transfers between devices: 68.6 us -> 0.68 us
    all_gather x4 -> x0, blocking collectives: 36.6 us -> none  [the longest x2 18.8 us: on_device(): lax.all_gather(keys_own, 'seq', axis=0, tiled=True)]
    ppermute x0 -> x16, waiting for transfers between devices: none -> 34.5 us  [the longest x1 14.9 us: on_device(): lax.ppermute(grad_kv[:, rows_chip:].astype(BF16), 'row', flip).astype(F32)]
    all_gather x7 -> x5, waiting for transfers between devices: 363 us -> 346 us  [gather(): return lax.all_gather(block, CHIPS, axis=0, tiled=True)]
  transfers between devices with their start and end apart: 18 -> 26, of which waited for: 17 -> 18; matrix products, arithmetic and copies ran while one was open for 12% -> 13% of each run, Pallas kernels for 0% -> 0%
where the time goes in v1:
time: 1250 us; the launch traced here: 1240 us
  waiting for transfers between devices  993 us (79%)
  matrix products  122 us (10%)
  local copies, waits for them, and re-layouts  51.8 us (4%)
  other arithmetic  48.6 us (4%)
  between operations  15.6 us (1%)
    reduce_scatter x5, waiting for transfers between devices, scatter(): lax.psum_scatter(grad.astype(BF16), CHIPS, scatter_dimension=0, tiled=True)  612 us
    all_gather x5, waiting for transfers between devices, gather(): return lax.all_gather(block, CHIPS, axis=0, tiled=True)  346 us
    dot_general x15, matrix products, dot(): lax.dot_general(left, right, (((left_dim,), (right_dim,)), ((), ())), pre...  95.6 us
  transfers between devices with their start and end apart: 26, of which 18 were waited for; matrix products, arithmetic and copies ran while one was open for 13% of the time, Pallas kernels for 0%

profile of v1, /device:TPU:0, one launch (start us, length us, event | category | flops | bytes accessed | tf_op | source)
XLA Modules:
  0.0 1239.2 jit_solution(12100864284088302083)
XLA Ops:
  15.4 4.6 dynamic-slice_reduce_fusion.2
  29.0 67.1 %all-gather.6.cloned.1.call-done = bf16[1536,1536]{1,0:T(8,128)(2,1)} async-done(((bf16[96,1536]{1,0:T(8,128)(2,1)}), bf16[1536,1536]{1,0:T(8,128)(2,1)}) %all-gather.6.cloned.1.call-update) | async-done | bytes 4718608 | tf_op jit(solution)/shard_map/all_gather | solution.py:122
  96.1 4.5 fusion.7
  110.1 12.8 %collective-permute-done.2 = bf16[2,256,768]{2,1,0:T(8,128)(2,1)} collective-permute-done((bf16[2,256,768]{2,1,0:T(8,128)(2,1)}, bf16[2,256,768]{2,1,0:T(8,128)(2,1)}, u32[]{:S(2)}, u32[]{:S(2)}) %collective-permute-start.2) | collective-permute-done | bytes 786464 | tf_op jit(solution)/shard_map/ppermute | solution.py:199
  127.8 5.5 fusion.90
  133.3 4.2 fusion.45
  138.6 22.6 %all-gather.8.cloned.1.call-done = bf16[1536,768]{1,0:T(8,128)(2,1)} async-done(((bf16[96,768]{1,0:T(8,128)(2,1)}), bf16[1536,768]{1,0:T(8,128)(2,1)}) %all-gather.8.cloned.1.call-update) | async-done | bytes 2359312 | tf_op jit(solution)/shard_map/all_gather | solution.py:122
  171.4 84.4 %all-gather.12.cloned.1.call-done = bf16[1536,2048]{1,0:T(8,128)(2,1)} async-done(((bf16[96,2048]{1,0:T(8,128)(2,1)}), bf16[1536,2048]{1,0:T(8,128)(2,1)}) %all-gather.12.cloned.1.call-update) | async-done | bytes 6291472 | tf_op jit(solution)/shard_map/all_gather | solution.py:122
  255.9 8.6 fusion.98
  264.5 86.1 %all-gather.10.cloned.1.call-done = bf16[1536,2048]{1,0:T(8,128)(2,1)} async-done(((bf16[96,2048]{1,0:T(8,128)(2,1)}), bf16[1536,2048]{1,0:T(8,128)(2,1)}) %all-gather.10.cloned.1.call-update) | async-done | bytes 6291472 | tf_op jit(solution)/shard_map/all_gather | solution.py:122
  350.6 8.6 fusion.97
  359.2 86.0 %all-gather.14.cloned.1.call-done = bf16[2048,1536]{1,0:T(8,128)(2,1)} async-done(((bf16[128,1536]{1,0:T(8,128)(2,1)}), bf16[2048,1536]{1,0:T(8,128)(2,1)}) %all-gather.14.cloned.1.call-update) | async-done | bytes 6291472 | tf_op jit(solution)/shard_map/all_gather | solution.py:122
  445.2 12.1 multiply_convert_fusion
  460.8 5.8 fusion.96
  477.2 4.9 convolution_convert_fusion.5
  482.1 4.8 reshape.611
  490.4 6.2 fusion.16
  499.8 5.2 fusion.1
  505.0 4.9 fusion.3
  524.0 14.9 %collective-permute-done.10 = bf16[2,256,768]{2,1,0:T(8,128)(2,1)S(1)} collective-permute-done((bf16[2,256,768]{2,1,0:T(8,128)(2,1)S(1)}, bf16[2,256,768]{2,1,0:T(8,128)(2,1)S(1)}, u32[]{:S(2)}, u32[]{:S(2)}) %collective-permute-start.10) | collective-permute-done | bytes 786464 | tf_op jit(solution)/shard_map/ppermute | solution.py:265
  547.0 5.3 convolution_convert_fusion.3
  552.4 8.2 convolution_convert_fusion.1
  561.2 8.2 convolution_convert_fusion.2
  569.4 8.3 convolution_convert_fusion
  577.7 6.4 fusion.99
  590.0 5.1 fusion.5
  599.8 27.8 %reduce-scatter.8.cloned.1.call-done = bf16[96,768]{1,0:T(8,128)(2,1)} async-done(((bf16[1536,768]{1,0:T(8,128)(2,1)}), bf16[96,768]{1,0:T(8,128)(2,1)}) %reduce-scatter.8.cloned.1.call-update) | async-done | bytes 147472 | tf_op jit(solution)/shard_map/reduce_scatter | solution.py:225
  628.6 3.8 fusion.22
  633.2 137.8 %reduce-scatter.6.cloned.1.call-done = bf16[96,1536]{1,0:T(8,128)(2,1)} async-done(((bf16[1536,1536]{1,0:T(8,128)(2,1)}), bf16[96,1536]{1,0:T(8,128)(2,1)}) %reduce-scatter.6.cloned.1.call-update) | async-done | bytes 294928 | tf_op jit(solution)/shard_map/reduce_scatter | solution.py:225
  775.2 147.1 %reduce-scatter.12.cloned.1.call-done = bf16[96,2048]{1,0:T(8,128)(2,1)} async-done(((bf16[1536,2048]{1,0:T(8,128)(2,1)}), bf16[96,2048]{1,0:T(8,128)(2,1)}) %reduce-scatter.12.cloned.1.call-update) | async-done | bytes 393232 | tf_op jit(solution)/shard_map/reduce_scatter | solution.py:225
  924.8 149.1 %reduce-scatter.10.cloned.1.call-done = bf16[96,2048]{1,0:T(8,128)(2,1)} async-done(((bf16[1536,2048]{1,0:T(8,128)(2,1)}), bf16[96,2048]{1,0:T(8,128)(2,1)}) %reduce-scatter.10.cloned.1.call-update) | async-done | bytes 393232 | tf_op jit(solution)/shard_map/reduce_scatter | solution.py:225
  1075.1 150.1 %reduce-scatter.14.cloned.1.call-done = bf16[128,1536]{1,0:T(8,128)(2,1)} async-done(((bf16[2048,1536]{1,0:T(8,128)(2,1)}), bf16[128,1536]{1,0:T(8,128)(2,1)}) %reduce-scatter.14.cloned.1.call-update) | async-done | bytes 393232 | tf_op jit(solution)/shard_map/reduce_scatter | solution.py:225
  (292 shorter events, 112.5 us)
Async XLA Ops:
  7.2 88.9 %all-gather.6.cloned.1.call-start = ((), (), s32[]{:S(2)}) async-start(), calls=%async_computation.5 | async-start | bytes 5013504 | tf_op jit(solution)/shard_map/all_gather | solution.py:122
  11.1 1.7 collective-permute-start.1
  13.6 147.6 %all-gather.8.cloned.1.call-start = ((), (), s32[]{:S(2)}) async-start(), calls=%async_computation.6 | async-start | bytes 2506752 | tf_op jit(solution)/shard_map/all_gather | solution.py:122
  14.3 241.6 %all-gather.12.cloned.1.call-start = ((), (), s32[]{:S(2)}) async-start(), calls=%async_computation.8 | async-start | bytes 6684672 | tf_op jit(solution)/shard_map/all_gather | solution.py:122
  20.2 1.8 collective-permute-start.5
  23.2 327.4 %all-gather.10.cloned.1.call-start = ((), (), s32[]{:S(2)}) async-start(), calls=%async_computation.7 | async-start | bytes 6684672 | tf_op jit(solution)/shard_map/all_gather | solution.py:122
  23.8 421.5 %all-gather.14.cloned.1.call-start = ((), (), s32[]{:S(2)}) async-start(), calls=%async_computation.9 | async-start | bytes 6684672 | tf_op jit(solution)/shard_map/all_gather | solution.py:122
  23.8 141.2 %collective-permute-start.7 = (bf16[2,128,1536]{2,1,0:T(8,128)(2,1)}, bf16[2,128,1536]{2,1,0:T(8,128)(2,1)}, u32[]{:S(2)}, u32[]{:S(2)}) collective-permute-start(bf16[2,128,1536]{2,1,0:T(8,128)(2,1)} %bitcast.43), channel_id=1, source_target_pairs={{0,1},{1,0},{2,3},{3,2},{4,5},{5,4},{6,7},{7,6},{8,9},{9,8},{10,11... | collective-permute-start | bytes 2359304 | tf_op jit(solution)/shard_map/ppermute | solution.py:55
  24.3 3.8 collective-permute-start
  24.4 603.2 %reduce-scatter.8.cloned.1.call-start = ((), (), s32[]{:S(2)}) async-start(), calls=%async_computation.11 | async-start | bytes 2506752 | tf_op jit(solution)/shard_map/reduce_scatter | solution.py:225
  28.0 74.6 %copy-start.23 = (f32[2,256,48]{1,2,0:T(8,128)}, f32[2,256,48]{1,2,0:T(8,128)S(1)}, u32[]{:S(2)}) copy-start(f32[2,256,48]{1,2,0:T(8,128)S(1)} %get-tuple-element.111) | copy-start | bytes 294916
  28.0 74.6 %copy-start.33 = (f32[2,256,48]{1,2,0:T(8,128)}, f32[2,256,48]{1,2,0:T(8,128)S(1)}, u32[]{:S(2)}) copy-start(f32[2,256,48]{1,2,0:T(8,128)S(1)} %get-tuple-element.110) | copy-start | bytes 294916
  104.0 18.9 %collective-permute-start.2 = (bf16[2,256,768]{2,1,0:T(8,128)(2,1)}, bf16[2,256,768]{2,1,0:T(8,128)(2,1)}, u32[]{:S(2)}, u32[]{:S(2)}) collective-permute-start(bf16[2,256,768]{2,1,0:T(8,128)(2,1)} %pad_maximum_fusion.6), channel_id=1, source_target_pairs={{0,2},{2,0},{1,3},{3,1},{4,6},{6,4},{5,7},{7,5},{8,10},{10,8},{9,1... | collective-permute-start | bytes 2359304 | tf_op jit(solution)/shard_map/ppermute | solution.py:199
  164.4 3.3 collective-permute-start.3
  164.5 3.4 collective-permute-start.4
  466.7 2.4 collective-permute-start.8
  466.8 3.4 collective-permute-start.9
  499.8 271.2 %reduce-scatter.6.cloned.1.call-start = ((), (), s32[]{:S(2)}) async-start(), calls=%async_computation.10 | async-start | bytes 5013504 | tf_op jit(solution)/shard_map/reduce_scatter | solution.py:225
  517.2 21.7 %collective-permute-start.10 = (bf16[2,256,768]{2,1,0:T(8,128)(2,1)S(1)}, bf16[2,256,768]{2,1,0:T(8,128)(2,1)S(1)}, u32[]{:S(2)}, u32[]{:S(2)}) collective-permute-start(bf16[2,256,768]{2,1,0:T(8,128)(2,1)S(1)} %fusion.27), channel_id=1, source_target_pairs={{0,2},{2,0},{1,3},{3,1},{4,6},{6,4},{5,7},{7,5},{8,10},{10,8},{9,1... | collective-permute-start | bytes 2359304 | tf_op jit(solution)/shard_map/ppermute | solution.py:265
  552.4 369.9 %reduce-scatter.12.cloned.1.call-start = ((), (), s32[]{:S(2)}) async-start(), calls=%async_computation.13 | async-start | bytes 6684672 | tf_op jit(solution)/shard_map/reduce_scatter | solution.py:225
  560.7 513.2 %reduce-scatter.10.cloned.1.call-start = ((), (), s32[]{:S(2)}) async-start(), calls=%async_computation.12 | async-start | bytes 6684672 | tf_op jit(solution)/shard_map/reduce_scatter | solution.py:225
  569.4 655.9 %reduce-scatter.14.cloned.1.call-start = ((), (), s32[]{:S(2)}) async-start(), calls=%async_computation.14 | async-start | bytes 6684672 | tf_op jit(solution)/shard_map/reduce_scatter | solution.py:225
  586.8 9.0 collective-permute-start.6
  595.2 3.7 collective-permute-start.11
  628.5 3.9 collective-permute-start.13
  628.6 144.8 %copy-start.40 = (bf16[48,768]{1,0:T(8,128)(2,1)S(1)}, bf16[48,768]{1,0:T(8,128)(2,1)}, u32[]{:S(2)}) copy-start(bf16[48,768]{1,0:T(8,128)(2,1)} %param.15) | copy-start | bytes 221188
  628.6 144.8 %copy-start.41 = (bf16[48,768]{1,0:T(8,128)(2,1)S(1)}, bf16[48,768]{1,0:T(8,128)(2,1)}, u32[]{:S(2)}) copy-start(bf16[48,768]{1,0:T(8,128)(2,1)} %param.16) | copy-start | bytes 221188
  628.6 144.8 %copy-start.44 = (f32[48]{0:T(128)S(1)}, f32[48]{0:T(128)}, u32[]{:S(2)}) copy-start(f32[48]{0:T(128)} %copy-done.43) | copy-start | bytes 580
  632.4 141.9 %copy-start.38 = (bf16[48,1536]{1,0:T(8,128)(2,1)S(1)}, bf16[48,1536]{1,0:T(8,128)(2,1)}, u32[]{:S(2)}) copy-start(bf16[48,1536]{1,0:T(8,128)(2,1)} %param.14) | copy-start | bytes 442372
  772.0 1.4 collective-permute-start.12
  923.4 303.8 %collective-permute-start.15 = (bf16[48,2048]{1,0:T(8,128)(2,1)S(1)}, bf16[48,2048]{1,0:T(8,128)(2,1)S(1)}, u32[]{:S(2)}, u32[]{:S(2)}) collective-permute-start(bf16[48,2048]{1,0:T(8,128)(2,1)S(1)} %get-tuple-element.86), channel_id=1, source_target_pairs={{0,1},{1,0},{2,3},{3,2},{4,5},{5,4},{6,7},{7,6},{8,9},{9,8},{10,11... | collective-permute-start | bytes 589832 | tf_op jit(solution)/shard_map/ppermute | solution.py:55
  1075.0 153.6 %collective-permute-start.14 = (bf16[48,2048]{1,0:T(8,128)(2,1)S(1)}, bf16[48,2048]{1,0:T(8,128)(2,1)S(1)}, u32[]{:S(2)}, u32[]{:S(2)}) collective-permute-start(bf16[48,2048]{1,0:T(8,128)(2,1)S(1)} %get-tuple-element.88), channel_id=1, source_target_pairs={{0,1},{1,0},{2,3},{3,2},{4,5},{5,4},{6,7},{7,6},{8,9},{9,8},{10,11... | collective-permute-start | bytes 589832 | tf_op jit(solution)/shard_map/ppermute | solution.py:55
  (49 other events, 364.5 us)
Sparse Core Ops, SparseCore 0:
  13.7 82.3 all-gather.5
  99.5 61.6 all-gather.7
  164.1 91.7 all-gather.11
  258.6 91.9 all-gather.9
  353.3 91.9 all-gather.13
  499.9 127.6 reduce-scatter.7
  632.8 138.1 reduce-scatter.5
  776.2 146.1 reduce-scatter.11
  927.6 146.2 reduce-scatter.9
  1079.0 146.2 reduce-scatter.13
